TPU v7x, 32 devices: a whole 2x2x4 slice. The times are simulated.
32 devices in a mesh: row: 8 (over z, core), col: 4 (over y, x).
Axes of the slice: x: 2, y: 2, z: 4, core: 2. Of those that a mesh axis runs over, the one named last changes fastest.
Arguments:
- grm_prior: float32 [1024, 1024], P('row', 'col'), may hold values from -0.6 to 0.6
- dosage_now: bfloat16 [1024, 4096], P('row', 'col'), may hold values from 0 to 2
- mask_now: int32 [1024, 4096], P('row', 'col'), may hold values 0 or 1
- dosage_prev: bfloat16 [1024, 256], P('row'), may hold values from 0 to 2
- mask_prev: int32 [1024, 256], P('row'), may hold values 0 or 1
- expression: bfloat16 [1024, 20480], P('row', 'col'), may hold values from -18 to 18
Outputs:
- grm_total: float32 [1024, 1024], P('row', 'col')
- assoc_score: float32 [256, 20480], P('row', 'col')
All inputs are finite; a program needn't handle non-finite values. No bound on the sum of `mask_now` or of `mask_prev` on one device may be relied on, other than what follows from the above.
Results may differ from a plain program's by a relative error of at most 0.0029.
Values may be sent and summed in bfloat16 or wider, within the bound.
A program may use at most 64 MiB of HBM per device.

v0:
```python
import math
import jax
import jax.numpy as jnp
from jax import lax
from jax.sharding import PartitionSpec as P

VARIANTS = 4096
epsilon = 1e-05


def spread(value, axis, source):
    kept = jnp.where(lax.axis_index(axis) == source, value, 0).astype(value.dtype)
    return lax.psum(kept, axis)


def local_sums(dosage, present):
    values = dosage.astype(jnp.float32)
    weight = present.astype(jnp.float32)
    return (values, weight, jnp.sum(weight, 0), jnp.sum(weight * values, 0))


def body(grm_prior, dosage_now, mask_now, dosage_prev, mask_prev, expression):
    samples_all = dosage_now.shape[0] * lax.axis_size("row")
    values_now, weight_now, seen_now, summed_now = local_sums(dosage_now, mask_now)
    values_prev, weight_prev, seen_prev, summed_prev = local_sums(dosage_prev, mask_prev)
    traits = expression.astype(jnp.float32)
    squares_trait = jnp.sum(traits * traits, 0)
    seen_now, summed_now, seen_prev, summed_prev, squares_trait = lax.psum(
        (seen_now, summed_now, seen_prev, summed_prev, squares_trait), "row"
    )
    observed_now = jnp.maximum(seen_now, 1.0)
    observed_prev = jnp.maximum(seen_prev, 1.0)
    offset_now = weight_now * (values_now - summed_now / observed_now)
    offset_prev = weight_prev * (values_prev - summed_prev / observed_prev)
    second_now, second_prev = lax.psum(
        (jnp.sum(offset_now * offset_now, 0), jnp.sum(offset_prev * offset_prev, 0)), "row"
    )
    spread_now = second_now / observed_now
    spread_prev = second_prev / observed_prev
    scaled = (offset_now * lax.rsqrt(spread_now + epsilon)).astype(jnp.bfloat16)
    own_panel = lax.all_gather(scaled, "col", axis=1, tiled=True)
    panels = lax.axis_size("row") // lax.axis_size("col")
    column = lax.axis_index("col")
    blocks = []
    for member in range(panels):
        remote = spread(own_panel, "row", column * panels + member)
        blocks.append(
            lax.dot_general(
                own_panel, remote, (((1,), (1,)), ((), ())), preferred_element_type=jnp.float32
            )
        )
    grm_total = grm_prior + jnp.concatenate(blocks, 1) / VARIANTS
    genotype = offset_prev.astype(jnp.bfloat16)
    out_rows = genotype.shape[1] // lax.axis_size("row")
    first_row = lax.axis_index("row") * out_rows
    cross_sum = lax.psum_scatter(
        lax.dot_general(
            genotype, expression, (((0,), (0,)), ((), ())), preferred_element_type=jnp.float32
        ),
        "row",
        scatter_dimension=0,
        tiled=True,
    )
    spread_rows = lax.dynamic_slice_in_dim(spread_prev, first_row, out_rows, 0)
    power = squares_trait / samples_all
    assoc_score = (
        cross_sum
        * lax.rsqrt(spread_rows + epsilon)[:, None]
        * lax.rsqrt(power + epsilon)[None, :]
        / math.sqrt(samples_all)
    )
    return (grm_total, assoc_score)


def solution(mesh):
    in_specs = (
        P("row", "col"),
        P("row", "col"),
        P("row", "col"),
        P("row", None),
        P("row", None),
        P("row", "col"),
    )
    out_specs = (P("row", "col"), P("row", "col"))
    return jax.shard_map(body, mesh=mesh, in_specs=in_specs, out_specs=out_specs, check_vma=False)
```

profile of v0, /device:TPU:0, one launch (start us, length us, event | category | flops | bytes accessed | tf_op | source)
XLA Modules:
  0.0 232.5 jit_solution(1334787050042367653)
XLA Ops:
  7.2 0.0 copy-start.2
  7.2 0.0 copy-start.4
  7.2 0.0 copy-start.1
  7.2 0.0 all-gather.2.cloned.1.call-start
  7.2 1.3 convert_reduce_fusion
  8.6 0.0 copy-start.3
  8.6 1.0 convert_reduce_fusion.1
  9.6 30.3 %all-reduce.1 = (f32[1024]{0:T(1024)S(1)}, f32[1024]{0:T(1024)S(1)}, f32[256]{0:T(256)S(1)}, f32[256]{0:T(256)S(1)}) all-reduce(f32[1024]{0:T(1024)S(1)} %get-tuple-element.5, f32[1024]{0:T(1024)S(1)} %get-tuple-element.4, f32[256]{0:T(256)S(1)} %get-tuple-element.7, ...), channel_id=1, replica_groups=mesh['row'=8,'col'=4] {'row'}, use_global_device_ids=true, to_apply=%region_1.0 | all-reduce | flops 2560 | bytes 20480 | tf_op jit(solution)/shard_map/psum | solution.py:28
  39.9 0.0 copy-done.2
  39.9 1.1 multiply_reduce_fusion.1
  41.0 0.0 copy-done.4
  41.0 0.9 multiply_reduce_fusion.2
  41.9 0.0 copy-done.1
  41.9 0.3 multiply_reduce_fusion
  42.2 26.0 %all-reduce = (f32[1024]{0:T(1024)S(1)}, f32[5120]{0:T(1024)S(1)}, f32[256]{0:T(256)S(1)}) all-reduce(f32[1024]{0:T(1024)S(1)} %multiply_reduce_fusion.1, f32[5120]{0:T(1024)S(1)} %multiply_reduce_fusion, f32[256]{0:T(256)S(1)} %multiply_reduce_fusion.2), channel_id=1, replica_groups=mesh['row'=8,'col'=4] {'row'}, use_global_device_ids=true, to_apply=%region_5.0 | all-reduce | flops 6400 | bytes 51200 | tf_op jit(solution)/shard_map/psum | solution.py:35
  68.2 0.0 copy-done.3
  68.2 0.8 multiply_convert_fusion
  69.0 0.0 all-gather.2.cloned.1.call-update
  69.0 0.0 all-reduce.5.cloned.1.call-start
  69.1 24.8 %all-gather.2.cloned.1.call-done = bf16[128,4096]{1,0:T(8,128)(2,1)} async-done(((bf16[128,1024]{1,0:T(8,128)(2,1)}), bf16[128,4096]{1,0:T(8,128)(2,1)}) %all-gather.2.cloned.1.call-update) | async-done | bytes 1048592 | tf_op jit(solution)/shard_map/all_gather | solution.py:41
  93.9 2.8 %broadcast_select_fusion.1 = (bf16[128,4096]{1,0:T(8,128)(2,1)}, bf16[128,4096]{1,0:T(8,128)(2,1)}) fusion(bf16[128,4096]{1,0:T(8,128)(2,1)} %all-gather.2.cloned.1.call-done, pred[]{:T(512)S(6)} %eq.6, pred[]{:T(512)S(6)} %eq.7), kind=kLoop, calls=%fused_computation.2 | loop fusion | flops 1048576 | bytes 3145730 | tf_op jit(solution)/shard_map/jit(_where)/select_n | solution.py:12
  96.6 0.0 copy-start.6
  96.6 0.0 all-reduce.5.cloned.1.call-update
  96.7 0.0 reduce-scatter.2.cloned.1.call-start
  96.7 0.8 copy-done.6
  97.5 3.2 %fusion.6 = f32[256,5120]{1,0:T(8,128)} fusion(bf16[128,5120]{1,0:T(8,128)(2,1)S(1)} %copy-done.1, bf16[128,256]{1,0:T(8,128)(2,1)S(1)} %copy-done.6, s32[128,256]{1,0:T(8,128)S(1)} %copy-done.4, f32[256]{0:T(256)S(1)} %maximum_divide_fusion.2), kind=kOutput, calls=%fused_computation.20 | convolution fusion | flops 335708160 | bytes 6751232 | tf_op jit(solution)/shard_map/dot_general | solution.py:57
  100.7 0.0 copy-start.7
  100.7 0.0 copy-start
  100.7 0.0 reduce-scatter.2.cloned.1.call-update
  100.7 0.9 copy-done.7
  101.6 0.1 copy.8
  101.7 0.1 add_rsqrt_fusion.2
  101.8 60.3 %all-reduce.5.cloned.1.call-done = (bf16[128,4096]{1,0:T(8,128)(2,1)}, bf16[128,4096]{1,0:T(8,128)(2,1)}) async-done(((bf16[128,4096]{1,0:T(8,128)(2,1)}, bf16[128,4096]{1,0:T(8,128)(2,1)}), (bf16[128,4096]{1,0:T(8,128)(2,1)}, bf16[128,4096]{1,0:T(8,128)(2,1)})) %all-reduce.5.cloned.1.call-update) | async-done | bytes 2097168 | tf_op jit(solution)/shard_map/psum | solution.py:13
  162.1 0.0 copy-start.5
  162.1 0.0 copy-done
  162.1 1.7 fusion.9
  163.8 0.0 copy-done.5
  163.8 0.5 fusion.10
  164.4 0.8 copy.9
  165.2 58.7 %reduce-scatter.2.cloned.1.call-done = f32[32,5120]{1,0:T(8,128)} async-done(((f32[256,5120]{1,0:T(8,128)}), f32[32,5120]{1,0:T(8,128)}) %reduce-scatter.2.cloned.1.call-update) | async-done | bytes 655376 | tf_op jit(solution)/shard_map/reduce_scatter | solution.py:56
  223.9 2.1 multiply_multiply_fusion
  (6 shorter events, 0.1 us)
Async XLA Ops:
  7.2 32.7 %copy-start.2 = (s32[128,1024]{1,0:T(8,128)S(1)}, s32[128,1024]{1,0:T(8,128)}, u32[]{:S(2)}) copy-start(s32[128,1024]{1,0:T(8,128)} %param.8) | copy-start | bytes 1572868
  7.2 33.8 %copy-start.4 = (s32[128,256]{1,0:T(8,128)S(1)}, s32[128,256]{1,0:T(8,128)}, u32[]{:S(2)}) copy-start(s32[128,256]{1,0:T(8,128)} %param.10) | copy-start | bytes 393220
  7.2 34.7 %copy-start.1 = (bf16[128,5120]{1,0:T(8,128)(2,1)S(1)}, bf16[128,5120]{1,0:T(8,128)(2,1)}, u32[]{:S(2)}) copy-start(bf16[128,5120]{1,0:T(8,128)(2,1)} %param.11) | copy-start | bytes 3932164
  7.2 86.7 %all-gather.2.cloned.1.call-start = ((), (), s32[]{:S(2)}) async-start(), calls=%async_computation.1 | async-start | bytes 1310720 | tf_op jit(solution)/shard_map/all_gather | solution.py:41
  8.6 59.6 %copy-start.3 = (bf16[128,1024]{1,0:T(8,128)(2,1)S(1)}, bf16[128,1024]{1,0:T(8,128)(2,1)}, u32[]{:S(2)}) copy-start(bf16[128,1024]{1,0:T(8,128)(2,1)} %param.7) | copy-start | bytes 786436
  69.0 93.1 %all-reduce.5.cloned.1.call-start = ((), (), s32[]{:S(2)}) async-start(), calls=%async_computation.3 | async-start | bytes 4194304 | tf_op jit(solution)/shard_map/psum | solution.py:13
  96.6 0.8 copy-start.6
  96.7 127.2 %reduce-scatter.2.cloned.1.call-start = ((), (), s32[]{:S(2)}) async-start(), calls=%async_computation.2 | async-start | bytes 5898240 | tf_op jit(solution)/shard_map/reduce_scatter | solution.py:56
  100.7 0.9 copy-start.7
  100.7 61.4 %copy-start = (bf16[128,4096]{1,0:T(8,128)(2,1)S(1)}, bf16[128,4096]{1,0:T(8,128)(2,1)}, u32[]{:S(2)}) copy-start(bf16[128,4096]{1,0:T(8,128)(2,1)} %all-gather.2.cloned.1.call-done) | copy-start | bytes 3145732
  162.1 1.8 copy-start.5
Sparse Core Ops, SparseCore 0:
  69.1 24.6 all-gather.1
  96.8 65.2 all-reduce.4
  164.4 59.4 reduce-scatter.1
where the time goes:
time: 233 us; the launch traced here: 232 us
  waiting for transfers between devices  144 us (62%)
  blocking collectives  56.3 us (24%)
  between operations  13.9 us (6%)
  other arithmetic  10.3 us (4%)
  matrix products  5.47 us (2%)
  local copies, waits for them, and re-layouts  2.51 us (1%)
    psum x1, waiting for transfers between devices, spread(): return lax.psum(kept, axis)  60.3 us
    reduce_scatter x1, waiting for transfers between devices, body(): lax.psum_scatter(lax.dot_general(genotype, expression, (((0,), (0,)), (()...  58.7 us
    psum x1, blocking collectives, body(): lax.psum((seen_now, summed_now, seen_prev, summed_prev, squares_trait), '...  30.3 us
    psum x1, blocking collectives, body(): lax.psum((jnp.sum(offset_now * offset_now, 0), jnp.sum(offset_prev * offs...  26 us
    all_gather x1, waiting for transfers between devices, body(): own_panel = lax.all_gather(scaled, 'col', axis=1, tiled=True)  24.8 us
  transfers between devices with their start and end apart: 3, of which 3 were waited for; matrix products, arithmetic and copies ran while one was open for 3% of the time, Pallas kernels for 0%

commit v1 on v0

--- a/solution.py
+++ b/solution.py
@@ -10,7 +10,7 @@
 
 def spread(value, axis, source):
     kept = jnp.where(lax.axis_index(axis) == source, value, 0).astype(value.dtype)
-    return lax.psum(kept, axis)
+    return jnp.sum(lax.all_gather(kept, axis), axis=0)
 
 
 def local_sums(dosage, present):

time: 233 us -> 310 us (1.33)
  waiting for transfers between devices: 144 us -> 212 us
  other arithmetic: 10.3 us -> 20.4 us
    all_gather x0 -> x2, waiting for transfers between devices: none -> 157 us  [spread(): return jnp.sum(lax.all_gather(kept, axis), axis=0)]
    psum x1 -> x0, waiting for transfers between devices: 60.3 us -> none  [spread(): return lax.psum(kept, axis)]
    reduce_scatter x1, waiting for transfers between devices: 58.7 us -> 32.9 us  [body(): lax.psum_scatter(lax.dot_general(genotype, expression, (((0,), (0,)), (()...]
    reduce_sum x0 -> x2, other arithmetic: none -> 9.9 us  [spread(): return jnp.sum(lax.all_gather(kept, axis), axis=0)]
    all_gather x1, waiting for transfers between devices: 24.8 us -> 21.5 us  [body(): own_panel = lax.all_gather(scaled, 'col', axis=1, tiled=True)]
  transfers between devices with their start and end apart: 3 -> 4, of which waited for: 3 -> 4; matrix products, arithmetic and copies ran while one was open for 3% -> 4% of each run, Pallas kernels for 0% -> 0%
where the time goes in v1:
time: 310 us
  waiting for transfers between devices  212 us (68%)
  blocking collectives  56.3 us (18%)
  other arithmetic  20.4 us (7%)
  between operations  15.8 us (5%)
  matrix products  4.05 us (1%)
    all_gather x2, waiting for transfers between devices, spread(): return jnp.sum(lax.all_gather(kept, axis), axis=0)  157 us
    reduce_scatter x1, waiting for transfers between devices, body(): lax.psum_scatter(lax.dot_general(genotype, expression, (((0,), (0,)), (()...  32.9 us
    psum x1, blocking collectives, body(): lax.psum((seen_now, summed_now, seen_prev, summed_prev, squares_trait), '...  30.3 us
    psum x1, blocking collectives, body(): lax.psum((jnp.sum(offset_now * offset_now, 0), jnp.sum(offset_prev * offs...  26 us
    all_gather x1, waiting for transfers between devices, body(): own_panel = lax.all_gather(scaled, 'col', axis=1, tiled=True)  21.5 us
    reduce_sum x2, other arithmetic, spread(): return jnp.sum(lax.all_gather(kept, axis), axis=0)  9.9 us
  transfers between devices with their start and end apart: 4, of which 4 were waited for; matrix products, arithmetic and copies ran while one was open for 4% of the time, Pallas kernels for 0%

profile of v1, /device:TPU:0, one launch (start us, length us, event | category | flops | bytes accessed | tf_op | source)
XLA Modules:
  0.0 309.5 jit_solution(14837297254893685724)
XLA Ops:
  8.0 0.0 copy-start.4
  8.0 0.0 copy-start.2
  8.0 0.0 copy-start.1
  8.0 0.0 copy-start.3
  8.0 0.0 copy-start.5
  8.1 0.0 all-gather.6.cloned.1.call-start
  8.1 1.1 convert_reduce_fusion.1
  9.2 1.2 convert_reduce_fusion
  10.4 30.3 %all-reduce.1 = (f32[1024]{0:T(1024)S(1)}, f32[1024]{0:T(1024)S(1)}, f32[256]{0:T(256)S(1)}, f32[256]{0:T(256)S(1)}) all-reduce(f32[1024]{0:T(1024)S(1)} %get-tuple-element.5, f32[1024]{0:T(1024)S(1)} %get-tuple-element.4, f32[256]{0:T(256)S(1)} %get-tuple-element.7, ...), channel_id=1, replica_groups=mesh['row'=8,'col'=4] {'row'}, use_global_device_ids=true, to_apply=%region_1.0 | all-reduce | flops 2560 | bytes 20480 | tf_op jit(solution)/shard_map/psum | solution.py:28
  40.7 1.0 multiply_reduce_fusion.2
  41.7 1.2 multiply_reduce_fusion.1
  42.9 0.0 copy-done.1
  43.0 0.3 multiply_reduce_fusion
  43.3 26.0 %all-reduce = (f32[1024]{0:T(1024)S(1)}, f32[5120]{0:T(1024)S(1)}, f32[256]{0:T(256)S(1)}) all-reduce(f32[1024]{0:T(1024)S(1)} %multiply_reduce_fusion.1, f32[5120]{0:T(1024)S(1)} %multiply_reduce_fusion, f32[256]{0:T(256)S(1)} %multiply_reduce_fusion.2), channel_id=1, replica_groups=mesh['row'=8,'col'=4] {'row'}, use_global_device_ids=true, to_apply=%region_5.0 | all-reduce | flops 6400 | bytes 51200 | tf_op jit(solution)/shard_map/psum | solution.py:35
  69.3 0.0 copy-done.2
  69.3 0.0 copy-done.3
  69.3 0.8 multiply_convert_fusion
  70.1 0.0 all-gather.6.cloned.1.call-update
  70.1 0.0 reduce-scatter.2.cloned.1.call-start
  70.2 0.0 copy-done.4
  70.2 0.0 copy-done.5
  70.2 3.2 %fusion.6 = f32[256,5120]{1,0:T(8,128)} fusion(bf16[128,5120]{1,0:T(8,128)(2,1)S(1)} %copy-done.1, bf16[128,256]{1,0:T(8,128)(2,1)S(1)} %copy-done.5, s32[128,256]{1,0:T(8,128)S(1)} %copy-done.4, f32[256]{0:T(256)S(1)} %maximum_divide_fusion.2), kind=kOutput, calls=%fused_computation.20 | convolution fusion | flops 335708160 | bytes 6751232 | tf_op jit(solution)/shard_map/dot_general | solution.py:57
  73.4 0.0 reduce-scatter.2.cloned.1.call-update
  73.4 0.0 all-gather.8.cloned.1.call-start
  73.5 0.0 copy-start.6
  73.5 21.5 %all-gather.6.cloned.1.call-done = bf16[128,4096]{1,0:T(8,128)(2,1)} async-done(((bf16[128,1024]{1,0:T(8,128)(2,1)}), bf16[128,4096]{1,0:T(8,128)(2,1)}) %all-gather.6.cloned.1.call-update) | async-done | bytes 1048592 | tf_op jit(solution)/shard_map/all_gather | solution.py:41
  95.0 2.7 broadcast_select_fusion.1
  97.7 0.0 all-gather.8.cloned.1.call-update
  97.7 0.0 all-gather.10.cloned.1.call-start
  97.7 0.5 all-gather.10.cloned.1.call-update
  98.3 0.0 copy-done.6
  98.3 0.1 copy.8
  98.4 0.1 add_rsqrt_fusion.2
  98.5 32.9 %reduce-scatter.2.cloned.1.call-done = f32[32,5120]{1,0:T(8,128)} async-done(((f32[256,5120]{1,0:T(8,128)}), f32[32,5120]{1,0:T(8,128)}) %reduce-scatter.2.cloned.1.call-update) | async-done | bytes 655376 | tf_op jit(solution)/shard_map/reduce_scatter | solution.py:56
  131.4 2.1 multiply_multiply_fusion
  133.5 79.9 %all-gather.8.cloned.1.call-done = bf16[1024,4096]{1,0:T(8,128)(2,1)} async-done(((bf16[128,4096]{1,0:T(8,128)(2,1)}), bf16[1024,4096]{1,0:T(8,128)(2,1)}) %all-gather.8.cloned.1.call-update) | async-done | bytes 8388624 | tf_op jit(solution)/shard_map/all_gather | solution.py:13
  213.3 4.9 %reduce_sum.90 = bf16[128,4096]{1,0:T(8,128)(2,1)S(1)} reduce(bf16[8,128,4096]{2,1,0:T(8,128)(2,1)} %bitcast.7, bf16[]{:T(256)} %constant.14.clone.1), dimensions={0}, to_apply=%region_6.0 | reduce | flops 3670016 | bytes 9437186 | tf_op jit(solution)/shard_map/reduce_sum | solution.py:13
  218.3 77.0 %all-gather.10.cloned.1.call-done = bf16[1024,4096]{1,0:T(8,128)(2,1)} async-done(((bf16[128,4096]{1,0:T(8,128)(2,1)}), bf16[1024,4096]{1,0:T(8,128)(2,1)}) %all-gather.10.cloned.1.call-update) | async-done | bytes 8388624 | tf_op jit(solution)/shard_map/all_gather | solution.py:13
  295.2 0.0 copy-start
  295.2 5.0 %reduce_sum.91 = bf16[128,4096]{1,0:T(8,128)(2,1)S(1)} reduce(bf16[8,128,4096]{2,1,0:T(8,128)(2,1)} %bitcast.8, bf16[]{:T(256)} %constant.14.clone.1), dimensions={0}, to_apply=%region_7.0 | reduce | flops 3670016 | bytes 9437186 | tf_op jit(solution)/shard_map/reduce_sum | solution.py:13
  300.2 0.0 copy-done
  300.2 0.4 fusion.9
  300.7 0.4 fusion.10
  301.2 0.8 copy.9
  (6 shorter events, 0.1 us)
Async XLA Ops:
  8.0 62.2 %copy-start.4 = (s32[128,256]{1,0:T(8,128)S(1)}, s32[128,256]{1,0:T(8,128)}, u32[]{:S(2)}) copy-start(s32[128,256]{1,0:T(8,128)} %param.10) | copy-start | bytes 393220
  8.0 61.3 %copy-start.2 = (s32[128,1024]{1,0:T(8,128)S(1)}, s32[128,1024]{1,0:T(8,128)}, u32[]{:S(2)}) copy-start(s32[128,1024]{1,0:T(8,128)} %param.8) | copy-start | bytes 1572868
  8.0 34.9 %copy-start.1 = (bf16[128,5120]{1,0:T(8,128)(2,1)S(1)}, bf16[128,5120]{1,0:T(8,128)(2,1)}, u32[]{:S(2)}) copy-start(bf16[128,5120]{1,0:T(8,128)(2,1)} %param.11) | copy-start | bytes 3932164
  8.0 61.2 %copy-start.3 = (bf16[128,1024]{1,0:T(8,128)(2,1)S(1)}, bf16[128,1024]{1,0:T(8,128)(2,1)}, u32[]{:S(2)}) copy-start(bf16[128,1024]{1,0:T(8,128)(2,1)} %param.7) | copy-start | bytes 786436
  8.0 62.1 %copy-start.5 = (bf16[128,256]{1,0:T(8,128)(2,1)S(1)}, bf16[128,256]{1,0:T(8,128)(2,1)}, u32[]{:S(2)}) copy-start(bf16[128,256]{1,0:T(8,128)(2,1)} %param.9) | copy-start | bytes 196612
  8.1 86.9 %all-gather.6.cloned.1.call-start = ((), (), s32[]{:S(2)}) async-start(), calls=%async_computation.1 | async-start | bytes 1310720 | tf_op jit(solution)/shard_map/all_gather | solution.py:41
  70.1 61.3 %reduce-scatter.2.cloned.1.call-start = ((), (), s32[]{:S(2)}) async-start(), calls=%async_computation.2 | async-start | bytes 5898240 | tf_op jit(solution)/shard_map/reduce_scatter | solution.py:56
  73.4 140.0 %all-gather.8.cloned.1.call-start = ((), (), s32[]{:S(2)}) async-start(), calls=%async_computation.3 | async-start | bytes 9437184 | tf_op jit(solution)/shard_map/all_gather | solution.py:13
  73.5 24.8 %copy-start.6 = (f32[128,256]{1,0:T(8,128)S(1)}, f32[128,256]{1,0:T(8,128)}, u32[]{:S(2)}) copy-start(f32[128,256]{1,0:T(8,128)} %param.6) | copy-start | bytes 393220
  97.7 197.5 %all-gather.10.cloned.1.call-start = ((), (), s32[]{:S(2)}) async-start(), calls=%async_computation.4 | async-start | bytes 9437184 | tf_op jit(solution)/shard_map/all_gather | solution.py:13
  295.2 5.0 %copy-start = (bf16[128,4096]{1,0:T(8,128)(2,1)S(1)}, bf16[128,4096]{1,0:T(8,128)(2,1)}, u32[]{:S(2)}) copy-start(bf16[128,4096]{1,0:T(8,128)(2,1)} %all-gather.6.cloned.1.call-done) | copy-start | bytes 3145732
Sparse Core Ops, SparseCore 0:
  70.2 24.6 all-gather.5
Sparse Core Ops, SparseCore 1:
  73.5 57.9 reduce-scatter.1
  132.9 80.4 all-gather.7
  214.8 80.4 all-gather.9
